TPU v7x, 512 devices: a whole 4x4x16 slice. The times are simulated.
512 devices in a mesh: flow: 128 (over z, x, core), leaf: 4 (over y).
Axes of the slice: x: 4, y: 4, z: 16, core: 2. Of those that a mesh axis runs over, the one named last changes fastest.
Arguments:
- vel_coef: float32 [81, 262144], P(None, 'flow'), may hold values from -6 to 6
- gp_block: int32 [1048576, 1], P(('flow', 'leaf')), may hold values from 0 to 127; in each aligned block of 2048 rows (0 to 2047, 2048 to 4095, ...) at most 32 rows name the same one
- gp_elem: int32 [1048576], P(('flow', 'leaf')), may hold values from 0 to 2047
- gp_param: float32 [3, 1048576], P(None, ('flow', 'leaf')), may hold values from 0 to 1
- gp_vel: float32 [3, 1048576], P(None, ('flow', 'leaf')), may hold values from -6 to 6
- gp_weight: float32 [1048576], P(('flow', 'leaf')), may hold values from 0.1 to 1
- gp_pos: float32 [3, 1048576], P(None, ('flow', 'leaf')), may hold values from -4 to 4
- contact_patch: int32 [1048576], P(('flow', 'leaf')), may hold values from 0 to 1023
- contact_param: float32 [2, 1048576], P(None, ('flow', 'leaf')), may hold values from 0 to 1
- patch_ctrl: float32 [27, 131072], P(None, ('flow', 'leaf')), may hold values from -4 to 4
Outputs:
- flow_force: float32 [81, 262144], P(None, ('flow', 'leaf'))
- shell_force: float32 [3, 1048576], P(None, ('flow', 'leaf'))
- patch_force: float32 [27, 131072], P(None, ('flow', 'leaf'))
Inputs may be any that keep to these rules, and one draw needn't show every extreme that they name: `gp_block`: the Gauss points of one device lie in at most 32 of each flow block's elements; some block is reached with exactly 32. `contact_patch`: A contact partner is one of the 1024 patches held by the Gauss point's own group, the devices of one index of flow.
All inputs are finite; a program needn't handle non-finite values.
Results may differ from a plain program's by a relative error of at most 0.0001.
Values sent between devices are 32-bit elements; how exact they have to be, the bound alone decides.
A program may use at most 64 MiB of HBM per device.

v0:
```python
import jax
import jax.numpy as jnp
from jax import lax
from jax.sharding import Mesh
from jax.sharding import PartitionSpec as P

FLOW = ("flow_0", "flow_1", "flow_2")
FLOW_LEAF = ("flow_0", "flow_1", "flow_2", "leaf")


BETA = 1.5
STIFF = 2.0
REACH = 0.5


def split_up(x, dim, size):
    before, after = (x.shape[:dim], x.shape[dim + 1 :])
    return jnp.moveaxis(x.reshape(*before, size, -1, *after), dim, 0)


def laid_out(pieces, dim):
    pieces = jnp.moveaxis(pieces, 0, dim)
    shape = pieces.shape
    return pieces.reshape(*shape[:dim], shape[dim] * shape[dim + 1], *shape[dim + 2 :])


def exchange_in_order(pieces, axes, turns):
    shape = [lax.axis_size(a) for a in axes]
    pieces = pieces.reshape(*shape, *pieces.shape[1:])
    for k in turns:
        pieces = lax.all_to_all(pieces, axes[k], split_axis=k, concat_axis=k, tiled=True)
    return pieces.reshape(-1, *pieces.shape[len(axes) :])


def exchange_by_chip(x, groups, turns, split_dim, concat_dim):
    size = lax.axis_size(groups[0]) * lax.axis_size(groups[1])
    pieces = split_up(x, split_dim, size)
    return laid_out(exchange_in_order(pieces, groups, turns), concat_dim)


def copy_for_each(x, axis):
    size = lax.axis_size(axis)
    return lax.all_to_all(jnp.broadcast_to(x[None], (size, *x.shape)), axis, 0, 0, tiled=True)


def collect(x, axis, dim):
    return laid_out(copy_for_each(x, axis), dim)


def sum_at_owner(x, axis, dim):
    size = lax.axis_size(axis)
    pieces = lax.all_to_all(split_up(x, dim, size), axis, 0, 0, tiled=True)
    return jnp.sum(pieces, axis=0)


def basis(x):
    return jnp.stack([0.5 * (1.0 - x) ** 2, 0.5 * (1.0 + 2.0 * x - 2.0 * x * x), 0.5 * x * x])


def solid_weights(param):
    first, second, third = (basis(param[0]), basis(param[1]), basis(param[2]))
    return (first[:, None, None, :] * second[None, :, None, :] * third[None, None, :, :]).reshape(
        27, -1
    )


def shell_weights(param):
    first, second = (basis(param[0]), basis(param[1]))
    return (first[:, None, :] * second[None, :, :]).reshape(9, -1)


def contact_force(position, partner_coef, weights):
    near = jnp.sum(partner_coef.reshape(3, 9, -1) * weights[None], axis=1)
    gap = position - near
    return STIFF * gap / (1.0 + jnp.sum(gap * gap, axis=0) / (REACH * REACH))


def decode(block, limit):
    flat = block.reshape(block.shape[0], -1)
    valid = flat[0] >= 0.0
    index = jnp.clip(flat[0].astype(jnp.int32), 0, limit - 1)
    return (flat, valid, index)


def take_columns(source, index):
    return jnp.transpose(jnp.transpose(source)[index])


def add_columns(columns, index, values):
    return jnp.transpose(
        jnp.zeros((columns, values.shape[0]), jnp.float32).at[index].add(jnp.transpose(values))
    )


def sample_flow(coef, index, weights):
    picked = take_columns(coef, index).reshape(3, 27, -1)
    return jnp.sum(picked * weights[None], axis=1)


def spread_rows(columns, index, weights, force):
    terms = (force[:, None, :] * weights[None]).reshape(81, -1)
    return add_columns(columns, index, terms)


def per_device(
    vel_coef,
    gp_block,
    gp_elem,
    gp_param,
    gp_vel,
    gp_weight,
    gp_pos,
    contact_patch,
    contact_param,
    patch_ctrl,
):
    owners = lax.axis_size(FLOW)
    peers = lax.axis_size("leaf")
    count = gp_elem.shape[0]
    slots_per = 2 * count // owners
    width = slots_per * owners
    elements = vel_coef.shape[1]
    dest = gp_block[:, 0]
    order = jnp.argsort(dest, stable=True)
    sorted_dest = dest[order]
    tally = jnp.sum(
        (dest[:, None] == jnp.arange(owners, dtype=jnp.int32)[None, :]).astype(jnp.int32), axis=0
    )
    starts = jnp.cumsum(tally) - tally
    rank_sorted = jnp.arange(count, dtype=jnp.int32) - starts[sorted_dest]
    slot = jnp.zeros((count,), jnp.int32).at[order].set(rank_sorted * owners + sorted_dest)

    def pack(values, filler):
        buffer = (
            jnp.full((width, values.shape[0]), filler, jnp.float32)
            .at[slot]
            .set(jnp.transpose(values))
        )
        return jnp.transpose(buffer).reshape(values.shape[0], slots_per, owners)

    elem_row = gp_elem.astype(jnp.float32)[None, :]
    payload = pack(jnp.concatenate([elem_row, gp_param, gp_vel, gp_weight[None, :]], axis=0), 0.0)
    occupied = pack(jnp.ones((1, count), jnp.float32), 0.0)
    payload = jnp.concatenate(
        [payload[:1] - (occupied < 0.5).astype(jnp.float32), payload[1:]], axis=0
    )
    block = lax.all_to_all(payload, FLOW, split_axis=2, concat_axis=2, tiled=True)
    flat, valid, index = decode(block, elements)
    speed = sample_flow(vel_coef, index, solid_weights(flat[1:4]))
    force = BETA * flat[7][None, :] * (flat[4:7] - speed) * valid[None, :].astype(jnp.float32)
    force = force.reshape(3, block.shape[1], block.shape[2])
    back = exchange_by_chip(force, (("flow_0", "flow_1"), "flow_2"), (1, 0), 2, 2)
    result = (back, force, block)
    back, arrived, kept = result
    fsi = take_columns(back.reshape(3, width), slot)
    flat, valid, index = decode(kept, elements)
    force = arrived.reshape(3, width) * valid[None, :].astype(jnp.float32)
    piece = collect(patch_ctrl, "leaf", 1)
    inside = (contact_patch >= 0) & (contact_patch < piece.shape[1])
    taken = take_columns(piece, jnp.clip(contact_patch, 0, piece.shape[1] - 1))
    partner_coef = jnp.where(inside[None, :], taken, jnp.zeros((27, count), jnp.float32))
    shell_w = shell_weights(contact_param)
    pushes = contact_force(gp_pos, partner_coef, shell_w)
    reaction = -(pushes[:, None, :] * shell_w[None]).reshape(27, -1)
    patch_term = add_columns(patch_ctrl.shape[1] * peers, contact_patch, reaction)
    partial_value = spread_rows(elements, index, solid_weights(flat[1:4]), force)
    flow_force, patch_force = (
        sum_at_owner(partial_value, "leaf", 1),
        sum_at_owner(patch_term, "leaf", 1),
    )
    shell_force = pushes - fsi
    return (flow_force, shell_force, patch_force)


def solution(mesh):
    split = Mesh(
        mesh.devices.reshape(16, 4, 2, mesh.shape["leaf"]), ("flow_0", "flow_1", "flow_2", "leaf")
    )
    placed = (
        P(None, FLOW),
        P(FLOW_LEAF, None),
        P(FLOW_LEAF),
        P(None, FLOW_LEAF),
        P(None, FLOW_LEAF),
        P(FLOW_LEAF),
        P(None, FLOW_LEAF),
        P(FLOW_LEAF),
        P(None, FLOW_LEAF),
        P(None, FLOW_LEAF),
    )
    return jax.shard_map(
        per_device,
        mesh=split,
        in_specs=placed,
        out_specs=(P(None, FLOW_LEAF), P(None, FLOW_LEAF), P(None, FLOW_LEAF)),
        check_vma=False,
    )
```

profile of v0, /device:TPU:1, one launch (start us, length us, event | category | flops | bytes accessed | tf_op | source)
XLA Modules:
  0.0 226.0 jit_solution(6742221681524914994)
XLA Ops:
  2.1 5.0 %all-to-all-start.2 = ((f32[4,27,256]{2,1,0:T(8,128)}), f32[4,27,256]{2,1,0:T(8,128)S(1)}, u32[]{:S(2)}, u32[]{:S(2)}) async-start(f32[4,27,256]{2,1,0:T(8,128)} %broadcast_in_dim.40), calls=%async_computation.2 | async-start | bytes 262144 | tf_op jit(solution)/shard_map/all_to_all | solution.py:43
  10.8 5.7 %sort.17 = (s32[2048]{0:T(1024)}, s32[2048]{0:T(1024)S(1)}) sort(s32[2048]{0:T(1024)} %bitcast.87, s32[2048]{0:T(1024)S(1)} %iota.11), dimensions={0}, to_apply=%region_0.0 | sort | flops 22528 | bytes 32768 | tf_op jit(solution)/shard_map/jit(argsort)/sort | solution.py:124
  16.6 11.8 %gather_fusion = s32[2048]{0:T(1024)S(1)} fusion(s32[2048]{0:T(1024)S(1)} %bitcast.88, s32[2048]{0:T(1024)S(1)} %get-tuple-element.59), kind=kCustom, calls=%fused_computation | custom fusion | bytes 24576 | tf_op jit(solution)/shard_map/gather | solution.py:125
  28.8 12.6 %gather_fusion.1 = s32[2048]{0:T(1024)S(1)} fusion(s32[128]{0:T(128)S(1)} %sub.116, s32[2048]{0:T(1024)S(1)} %broadcast_clamp_fusion.2), kind=kCustom, calls=%fused_computation.1 | custom fusion | bytes 24576 | tf_op jit(solution)/shard_map/gather | solution.py:130
  41.5 8.0 %scatter_custom_fusion = s32[2048]{0:T(1024)S(1)} fusion(s32[2048]{0:T(1024)S(1)} %get-tuple-element.60, s32[2048]{0:T(1024)S(1)} %multiply_add_fusion.6, s32[]{:T(128)} %constant.14.clone.1), kind=kCustom, calls=%fused_computation.98 | custom fusion | bytes 8196 | tf_op jit(solution)/shard_map/scatter | solution.py:131
  50.5 6.1 %scatter_custom_fusion.1 = f32[4096,8]{1,0:T(8,128)S(1)} fusion(s32[2048]{0:T(1024)S(1)} %get-tuple-element.58, f32[2048,8]{1,0:T(8,128)S(1)} %copy.187, f32[]{:T(128)} %constant.13.clone.1), kind=kCustom, calls=%fused_computation.15 | custom fusion | bytes 131076 | tf_op jit(solution)/shard_map/scatter | solution.py:137
  57.2 2.0 slice.80
  59.4 8.1 %scatter_custom_fusion.2 = f32[4096]{0:T(1024)S(1)} fusion(s32[2048]{0:T(1024)S(1)} %get-tuple-element.58, f32[2048]{0:T(1024)S(1)} %broadcast.353, f32[]{:T(128)} %constant.13.clone.1), kind=kCustom, calls=%fused_computation.87 | custom fusion | bytes 16388 | tf_op jit(solution)/shard_map/scatter | solution.py:137
  67.5 2.8 %copy.189 = f32[7,32,128]{1,0,2:T(8,128)S(1)} copy(f32[7,32,128]{0,2,1:T(8,128)} %bitcast.94) | data formatting | bytes 229376 | tf_op jit(solution)/shard_map/slice | solution.py:145
  71.8 19.9 %all-to-all-start = ((f32[128,1,256]{2,1,0:T(1,128)}), f32[128,1,256]{2,1,0:T(1,128)S(1)}, u32[]{:S(2)}, u32[]{:S(2)}) async-start(f32[128,1,256]{2,1,0:T(1,128)} %reshape.592), calls=%async_computation | async-start | bytes 262144 | tf_op jit(solution)/shard_map/all_to_all | solution.py:147
  91.9 5.5 %gather_fusion.3 = f32[2048,27]{1,0:T(8,128)S(1)} fusion(f32[1024,27]{1,0:T(8,128)S(1)} %bitcast.90, s32[2048]{0:T(1024)S(1)} %get-tuple-element.56), kind=kCustom, calls=%fused_computation.3 | custom fusion | bytes 450560 | tf_op jit(solution)/shard_map/gather | solution.py:86
  98.8 8.9 %all-to-all-done = f32[128,1,256]{2,1,0:T(1,128)S(1)} async-done(((f32[128,1,256]{2,1,0:T(1,128)}), f32[128,1,256]{2,1,0:T(1,128)S(1)}, u32[]{:S(2)}, u32[]{:S(2)}) %all-to-all-start) | async-done | bytes 131104 | tf_op jit(solution)/shard_map/all_to_all | solution.py:147
  113.0 10.8 %gather_fusion.2 = f32[4096,81]{1,0:T(8,128)S(1)} fusion(f32[2048,81]{1,0:T(8,128)S(1)} %bitcast.89, s32[4096]{0:T(1024)S(1)} %copy-done.5), kind=kCustom, calls=%fused_computation.2 | custom fusion | bytes 2670592 | tf_op jit(solution)/shard_map/gather | solution.py:86
  123.7 1.8 copy.194
  127.7 3.8 %all_to_all.30 = f32[2,1,6144]{2,1,0:T(1,128)S(1)} all-to-all(f32[2,1,6144]{2,1,0:T(1,128)S(1)} %reshape.594), channel_id=1, replica_groups=mesh['flow_0'=16,'flow_1'=4,'flow_2'=2,'leaf'=4] {'flow_2'}, dimensions={0} | all-to-all | bytes 98304 | tf_op jit(solution)/shard_map/all_to_all | solution.py:31
  133.5 6.3 %all-to-all-start.4 = ((f32[64,1,192]{2,1,0:T(1,128)}), f32[64,1,192]{2,1,0:T(1,128)S(1)}, u32[]{:S(2)}, u32[]{:S(2)}) async-start(f32[64,1,192]{2,1,0:T(1,128)} %reshape.596), calls=%async_computation.4 | async-start | bytes 131072 | tf_op jit(solution)/shard_map/all_to_all | solution.py:31
  139.8 13.9 %all-to-all-done.4 = f32[64,1,192]{2,1,0:T(1,128)S(1)} async-done(((f32[64,1,192]{2,1,0:T(1,128)}), f32[64,1,192]{2,1,0:T(1,128)S(1)}, u32[]{:S(2)}, u32[]{:S(2)}) %all-to-all-start.4) | async-done | bytes 49184 | tf_op jit(solution)/shard_map/all_to_all | solution.py:31
  154.8 1.9 copy.207
  156.8 7.6 %gather_fusion.4 = f32[2048,3]{1,0:T(8,128)} fusion(f32[4096,3]{1,0:T(8,128)S(1)} %bitcast.91, s32[2048]{0:T(1024)S(1)} %copy-done.9), kind=kCustom, calls=%fused_computation.4 | custom fusion | bytes 57344 | tf_op jit(solution)/shard_map/gather | solution.py:86
  167.0 11.7 %scatter_custom_fusion.4 = f32[1024,27]{1,0:T(8,128)S(1)} fusion(s32[2048]{0:T(1024)} %get-tuple-element.55, f32[2048,27]{1,0:T(8,128)S(1)} %copy.209, f32[]{:T(128)} %constant.13.clone.1), kind=kCustom, calls=%fused_computation.24 | custom fusion | flops 55296 | bytes 111104 | tf_op jit(solution)/shard_map/scatter-add | solution.py:91
  179.6 4.5 %all-to-all-start.5 = ((f32[4,27,256]{2,1,0:T(8,128)}), f32[4,27,256]{2,1,0:T(8,128)}, u32[]{:S(2)}, u32[]{:S(2)}) async-start(f32[4,27,256]{2,1,0:T(8,128)} %bitcast.40), calls=%async_computation.5 | async-start | bytes 262144 | tf_op jit(solution)/shard_map/all_to_all | solution.py:52
  185.2 26.5 %scatter_custom_fusion.3 = f32[2048,81]{1,0:T(8,128)S(1)} fusion(s32[4096]{0:T(1024)S(1)} %bitcast.113, f32[4096,81]{1,0:T(8,128)S(1)} %copy.198, f32[]{:T(128)} %constant.13.clone.1), kind=kCustom, calls=%fused_computation.19 | custom fusion | flops 331776 | bytes 663556 | tf_op jit(solution)/shard_map/scatter-add | solution.py:91
  212.9 4.1 %all-to-all-start.1 = ((f32[4,81,512]{2,1,0:T(8,128)}), f32[4,81,512]{2,1,0:T(8,128)S(1)}, u32[]{:S(2)}, u32[]{:S(2)}) async-start(f32[4,81,512]{2,1,0:T(8,128)} %bitcast.22), calls=%async_computation.1 | async-start | bytes 1441792 | tf_op jit(solution)/shard_map/all_to_all | solution.py:52
  218.5 6.8 %all-to-all-done.1 = f32[4,81,512]{2,1,0:T(8,128)S(1)} async-done(((f32[4,81,512]{2,1,0:T(8,128)}), f32[4,81,512]{2,1,0:T(8,128)S(1)}, u32[]{:S(2)}, u32[]{:S(2)}) %all-to-all-start.1) | async-done | bytes 663584 | tf_op jit(solution)/shard_map/all_to_all | solution.py:52
  (112 shorter events, 29.0 us)
Async XLA Ops:
  0.6 15.9 %copy-start = (s32[2048,1]{0,1:T(1,128)S(1)}, s32[2048,1]{0,1:T(1,128)}, u32[]{:S(2)}) copy-start(s32[2048,1]{0,1:T(1,128)} %param.11) | copy-start | bytes 24580
  2.1 69.7 %all-to-all-start.2 = ((f32[4,27,256]{2,1,0:T(8,128)}), f32[4,27,256]{2,1,0:T(8,128)S(1)}, u32[]{:S(2)}, u32[]{:S(2)}) async-start(f32[4,27,256]{2,1,0:T(8,128)} %broadcast_in_dim.40), calls=%async_computation.2 | async-start | bytes 262144 | tf_op jit(solution)/shard_map/all_to_all | solution.py:43
  28.8 21.3 %copy-start.6 = (f32[3,2048]{1,0:T(4,128)S(1)}, f32[3,2048]{1,0:T(4,128)}, u32[]{:S(2)}) copy-start(f32[3,2048]{1,0:T(4,128)} %param.14) | copy-start | bytes 73732
  28.8 21.3 %copy-start.7 = (f32[3,2048]{1,0:T(4,128)S(1)}, f32[3,2048]{1,0:T(4,128)}, u32[]{:S(2)}) copy-start(f32[3,2048]{1,0:T(4,128)} %param.13) | copy-start | bytes 73732
  28.8 21.3 %copy-start.11 = (f32[2048]{0:T(1024)S(1)}, f32[2048]{0:T(1024)}, u32[]{:S(2)}) copy-start(f32[2048]{0:T(1024)} %param.15) | copy-start | bytes 24580
  57.2 2.0 copy-start.10
  67.5 3.9 %copy-start.2 = (f32[81,2048]{1,0:T(8,128)S(1)}, f32[81,2048]{1,0:T(8,128)}, u32[]{:S(2)}) copy-start(f32[81,2048]{1,0:T(8,128)} %param.10) | copy-start | bytes 1990660
  71.8 35.9 %all-to-all-start = ((f32[128,1,256]{2,1,0:T(1,128)}), f32[128,1,256]{2,1,0:T(1,128)S(1)}, u32[]{:S(2)}, u32[]{:S(2)}) async-start(f32[128,1,256]{2,1,0:T(1,128)} %reshape.592), calls=%async_computation | async-start | bytes 262144 | tf_op jit(solution)/shard_map/all_to_all | solution.py:147
  97.3 0.8 copy-start.3
  111.5 1.5 copy-start.5
  125.5 1.6 copy-start.1
  127.1 12.7 %copy-start.4 = (f32[4096]{0:T(1024)S(1)}, f32[4096]{0:T(1024)}, u32[]{:S(2)}) copy-start(f32[4096]{0:T(1024)} %convert_bitcast_fusion.1) | copy-start | bytes 49156
  131.5 25.2 %copy-start.9 = (s32[2048]{0:T(1024)S(1)}, s32[2048]{0:T(1024)}, u32[]{:S(2)}) copy-start(s32[2048]{0:T(1024)} %get-tuple-element.57) | copy-start | bytes 24580
  133.5 20.3 %all-to-all-start.4 = ((f32[64,1,192]{2,1,0:T(1,128)}), f32[64,1,192]{2,1,0:T(1,128)S(1)}, u32[]{:S(2)}, u32[]{:S(2)}) async-start(f32[64,1,192]{2,1,0:T(1,128)} %reshape.596), calls=%async_computation.4 | async-start | bytes 131072 | tf_op jit(solution)/shard_map/all_to_all | solution.py:31
  156.7 9.1 %copy-start.8 = (f32[2048]{0:T(1024)S(1)}, f32[2048]{0:T(1024)}, u32[]{:S(2)}) copy-start(f32[2048]{0:T(1024)} %multiply_add_fusion.5) | copy-start | bytes 24580
  179.6 33.4 %all-to-all-start.5 = ((f32[4,27,256]{2,1,0:T(8,128)}), f32[4,27,256]{2,1,0:T(8,128)}, u32[]{:S(2)}, u32[]{:S(2)}) async-start(f32[4,27,256]{2,1,0:T(8,128)} %bitcast.40), calls=%async_computation.5 | async-start | bytes 262144 | tf_op jit(solution)/shard_map/all_to_all | solution.py:52
  212.9 12.4 %all-to-all-start.1 = ((f32[4,81,512]{2,1,0:T(8,128)}), f32[4,81,512]{2,1,0:T(8,128)S(1)}, u32[]{:S(2)}, u32[]{:S(2)}) async-start(f32[4,81,512]{2,1,0:T(8,128)} %bitcast.22), calls=%async_computation.1 | async-start | bytes 1441792 | tf_op jit(solution)/shard_map/all_to_all | solution.py:52
where the time goes:
time: 229 us; the launch traced here: 226 us
  local copies, waits for them, and re-layouts  94.2 us (41%)
  other arithmetic  57.6 us (25%)
  starting transfers between devices  39.7 us (17%)
  waiting for transfers between devices  29.6 us (13%)
  blocking collectives  3.82 us (2%)
    scatter-add x2, other arithmetic, add_columns(): jnp.zeros((columns, values.shape[0]), jnp.float32).at[index]  38.2 us
    gather x4, local copies, waits for them, and re-layouts, take_columns(): return jnp.transpose(jnp.transpose(source)[index])  25.4 us
    all_to_all x1, starting transfers between devices, per_device(): lax.all_to_all(payload, FLOW, split_axis=2, concat_axis=2, tiled=True)  19.9 us
    scatter x2, local copies, waits for them, and re-layouts, pack(): buffer = jnp.full((width, values.shape[0]), filler, jnp.float32).at[slot]...  14.2 us
    all_to_all x1, waiting for transfers between devices, exchange_in_order(): lax.all_to_all(pieces, axes[k], split_axis=k, concat_axis=k, tiled=True)  13.9 us
    gather x1, local copies, waits for them, and re-layouts, per_device(): rank_sorted = jnp.arange(count, dtype=jnp.int32) - starts[sorted_dest]  12.6 us
    gather x1, local copies, waits for them, and re-layouts, per_device(): sorted_dest = dest[order]  11.8 us
    all_to_all x1, waiting for transfers between devices, per_device(): lax.all_to_all(payload, FLOW, split_axis=2, concat_axis=2, tiled=True)  8.85 us
  transfers between devices with their start and end apart: 5, of which 3 were waited for; matrix products, arithmetic and copies ran while one was open for 45% of the time, Pallas kernels for 0%

commit v1 on v0

v1 whole, which is shorter than its diff:
```python
import functools

import jax
import jax.numpy as jnp
from jax import lax
from jax.experimental import pallas as pl
from jax.experimental.pallas import tpu as pltpu
from jax.sharding import PartitionSpec as P

BETA = 1.5
STIFF = 2.0
REACH = 0.5
CAP = 32
LANES = 128
F32 = jnp.float32
BF16 = jnp.bfloat16
MESH = pl.DeviceIdType.MESH
NT = (((1,), (1,)), ((), ()))


def split(x):
    high = x.astype(BF16)
    return high, (x - high.astype(F32)).astype(BF16)


def basis(x):
    return (0.5 * (1.0 - x) ** 2, 0.5 * (1.0 + 2.0 * x - 2.0 * x * x), 0.5 * x * x)


def pick(digit, values):
    return jnp.where(digit == 0, values[0], jnp.where(digit == 1, values[1], values[2]))


def one_hot(row, base, rows):
    step = min(rows, 256)
    number = lax.broadcasted_iota(jnp.int32, (step, LANES), 0).astype(F32).astype(BF16)
    one, zero = jnp.ones((step, LANES), BF16), jnp.zeros((step, LANES), BF16)
    out = []
    for first in range(0, rows, step):
        near = jnp.broadcast_to(row - float(base + first), (16, LANES)).astype(BF16)
        near = jnp.concatenate([near] * (step // 16), axis=0)
        out.append(jnp.where(number == near, one, zero))
    return jnp.concatenate(out, axis=0) if len(out) > 1 else out[0]


def kernel(
    vel_coef, dest_ref, elem_ref, param_ref, vel_ref, weight_ref, pos_ref, patch_ref, cparam_ref, ctrl_ref,
    flow_out, shell_out, patch_out,
    dest_hot, rank_row, packed, message, received, slots, coef, hot, terms, force_rows, answer, returned,
    contact_hot, contact_terms, push, ctrl_all, patch_part, patch_all, flow_part, flow_all,
    out_sem, back_sem, ctrl_sem, patch_sem, flow_sem,
):
    owners, peers = lax.axis_size("flow"), lax.axis_size("leaf")
    me, leaf = lax.axis_index("flow"), lax.axis_index("leaf")
    points = dest_ref.shape[1]
    elements = vel_coef.shape[1]
    per_leaf = elements // peers
    patches = ctrl_ref.shape[1]
    total_slots = CAP * owners

    def flow_peer(i):
        half = (i + 1) // 2
        return lax.rem(me + jnp.where(lax.rem(i, 2) == 0, owners // 2 + half, owners // 2 - half), owners)

    def leaf_peer(i):
        return lax.rem(leaf + 1 + i, peers)

    barrier = pltpu.get_barrier_semaphore()

    def greet(i, carry):
        pl.semaphore_signal(barrier, inc=1, device_id=(flow_peer(i), leaf), device_id_type=MESH)
        return carry

    lax.fori_loop(0, owners - 1, greet, 0)
    for i in range(peers - 1):
        pl.semaphore_signal(barrier, inc=1, device_id=(me, leaf_peer(i)), device_id_type=MESH)

    owner_number = lax.broadcasted_iota(jnp.int32, (owners, points), 0)
    dest_hot[...] = jnp.where(owner_number == dest_ref[...], 1.0, 0.0).astype(BF16)
    block = 256
    before = (
        lax.broadcasted_iota(jnp.int32, (block, block), 0) < lax.broadcasted_iota(jnp.int32, (block, block), 1)
    ).astype(F32).astype(BF16)
    carry = jnp.zeros((owners, 1), F32)
    for b in range(points // block):
        part = dest_hot[:, b * block : (b + 1) * block]
        ahead = jnp.dot(part, before, preferred_element_type=F32)
        wide = part.astype(F32)
        rank_row[:, b * block : (b + 1) * block] = jnp.sum(wide * (ahead + carry), axis=0, keepdims=True)
        carry = carry + jnp.sum(wide, axis=1, keepdims=True)

    rank_hot = lax.broadcasted_iota(jnp.int32, (CAP, points), 0).astype(F32) == rank_row[...]
    values = [elem_ref[...].astype(F32)]
    values += [param_ref[i : i + 1, :] for i in range(3)]
    values += [vel_ref[i : i + 1, :] for i in range(3)]
    values += [BETA * weight_ref[...]]
    for v, value in enumerate(values):
        high = value.astype(BF16).astype(F32)
        packed[v * CAP : (v + 1) * CAP, :] = jnp.where(rank_hot, high, 0.0).astype(BF16)
        packed[(8 + v) * CAP : (9 + v) * CAP, :] = jnp.where(rank_hot, value - high, 0.0).astype(BF16)
    spread = lax.dot_general(packed[...], dest_hot[...], NT, preferred_element_type=F32)
    spread = spread[: 8 * CAP] + spread[8 * CAP :]
    for h in range(2):
        message[pl.ds(h, owners, stride=2), :] = jnp.transpose(spread[h * LANES : (h + 1) * LANES])

    pl.semaphore_wait(barrier, owners - 1 + peers - 1)

    def out_copy(peer):
        return pltpu.make_async_remote_copy(
            src_ref=message.at[pl.ds(pl.multiple_of(2 * peer, 2), 2), :],
            dst_ref=received.at[pl.ds(pl.multiple_of(2 * me, 2), 2), :],
            send_sem=out_sem.at[0], recv_sem=out_sem.at[1],
            device_id=(peer, leaf), device_id_type=MESH,
        )

    def send_out(i, carry):
        out_copy(flow_peer(i)).start()
        return carry

    def ctrl_copy(peer):
        return pltpu.make_async_remote_copy(
            src_ref=ctrl_ref, dst_ref=ctrl_all.at[leaf], send_sem=ctrl_sem.at[0], recv_sem=ctrl_sem.at[1],
            device_id=(me, peer), device_id_type=MESH,
        )

    for i in range(peers - 1):
        ctrl_copy(leaf_peer(i)).start()
    lax.fori_loop(0, owners - 1, send_out, 0)
    mine = pl.ds(pl.multiple_of(2 * me, 2), 2)
    received[mine, :] = message[mine, :]
    ctrl_all[leaf] = ctrl_ref[...]

    coef[...] = jnp.zeros_like(coef)
    for c in range(3):
        high, low = split(vel_coef[c * 27 : (c + 1) * 27, :])
        coef[c * 32 : c * 32 + 27, :] = high
        coef[96 + c * 32 : 96 + c * 32 + 27, :] = low

    pltpu.make_async_remote_copy(
        src_ref=ctrl_all.at[: peers - 1], dst_ref=ctrl_all.at[: peers - 1], send_sem=ctrl_sem.at[0],
        recv_sem=ctrl_sem.at[1], device_id=(me, leaf_peer(0)), device_id_type=MESH,
    ).wait()
    zero7 = jnp.zeros((7, peers * patches), F32)
    whole = jnp.concatenate([ctrl_all[i] for i in range(peers)], axis=1)
    whole = jnp.concatenate([part for c in range(3) for part in (whole[c * 9 : (c + 1) * 9], zero7)], axis=0)
    ctrl_high, ctrl_low = split(whole)
    ctrl_terms = jnp.concatenate([ctrl_high, ctrl_low], axis=0)
    shell_k = lax.broadcasted_iota(jnp.int32, (16, 1), 0)
    contact_terms[...] = jnp.zeros_like(contact_terms)
    wide = 512
    for j in range(points // wide):
        cols = slice(j * wide, (j + 1) * wide)
        for i in range(wide // LANES):
            at = slice(j * wide + i * LANES, j * wide + (i + 1) * LANES)
            contact_hot[:, at] = one_hot(patch_ref[:, at].astype(F32), 0, peers * patches)
        taken = jnp.dot(ctrl_terms, contact_hot[:, cols], preferred_element_type=F32)
        taken = taken[:48] + taken[48:]
        weights = pick(shell_k // 3, basis(cparam_ref[0:1, cols])) * pick(
            lax.rem(shell_k, 3), basis(cparam_ref[1:2, cols])
        )
        weights = jnp.where(shell_k < 9, weights, 0.0)
        gap = [
            pos_ref[c : c + 1, cols] - jnp.sum(taken[c * 16 : (c + 1) * 16] * weights, axis=0, keepdims=True)
            for c in range(3)
        ]
        scale = STIFF / (1.0 + (gap[0] * gap[0] + gap[1] * gap[1] + gap[2] * gap[2]) / (REACH * REACH))
        for c in range(3):
            fc = scale * gap[c]
            push[c : c + 1, cols] = fc
            high, low = split(-(weights * fc))
            contact_terms[c * 16 : (c + 1) * 16, cols] = high
            contact_terms[64 + c * 16 : 64 + (c + 1) * 16, cols] = low
    reaction = lax.dot_general(contact_hot[...], contact_terms[...], NT, preferred_element_type=F32)
    reaction = jnp.transpose(reaction)
    reaction = reaction[:48] + reaction[64:112]
    for q in range(peers):
        for c in range(3):
            patch_part[q, c * 9 : (c + 1) * 9, :] = reaction[c * 16 : c * 16 + 9, q * patches : (q + 1) * patches]

    def patch_copy(peer):
        return pltpu.make_async_remote_copy(
            src_ref=patch_part.at[peer], dst_ref=patch_all.at[leaf], send_sem=patch_sem.at[0],
            recv_sem=patch_sem.at[1], device_id=(me, peer), device_id_type=MESH,
        )

    for i in range(peers - 1):
        patch_copy(leaf_peer(i)).start()
    patch_all[leaf] = patch_part[leaf]

    pltpu.make_async_remote_copy(
        src_ref=message.at[: 2 * (owners - 1), :], dst_ref=received.at[: 2 * (owners - 1), :],
        send_sem=out_sem.at[0], recv_sem=out_sem.at[1], device_id=(flow_peer(0), leaf), device_id_type=MESH,
    ).wait()
    for h in range(2):
        rows = jnp.transpose(received[pl.ds(h, owners, stride=2), :])
        for i in range(4):
            slots[4 * h + i] = rows[i * CAP : (i + 1) * CAP]
    solid_k = lax.broadcasted_iota(jnp.int32, (32, 1), 0)
    digits = (solid_k // 9, lax.rem(solid_k // 3, 3), lax.rem(solid_k, 3))
    force_rows[...] = jnp.zeros_like(force_rows)
    terms[96:128, :] = jnp.zeros((32, total_slots), BF16)
    terms[224:256, :] = jnp.zeros((32, total_slots), BF16)
    ranks = 4

    def owner_step(j, carry):
        cols = pl.ds(pl.multiple_of(j * ranks * LANES, ranks * LANES), ranks * LANES)
        hot[:, cols] = jnp.concatenate(
            [one_hot(slots[0, pl.ds(j * ranks + i, 1), :], 0, elements) for i in range(ranks)], axis=1
        )
        taken = jnp.dot(coef[...], hot[:, cols], preferred_element_type=F32)
        taken = taken[:96] + taken[96:]
        for i in range(ranks):
            r = j * ranks + i
            row = pl.ds(r, 1)
            weights = pick(digits[0], basis(slots[1, row, :]))
            weights = weights * pick(digits[1], basis(slots[2, row, :]))
            weights = weights * pick(digits[2], basis(slots[3, row, :]))
            weights = jnp.where(solid_k < 27, weights, 0.0)
            at = pl.ds(pl.multiple_of(r * LANES, LANES), LANES)
            for c in range(3):
                speed = jnp.sum(
                    taken[c * 32 : (c + 1) * 32, i * LANES : (i + 1) * LANES] * weights, axis=0, keepdims=True
                )
                force = slots[7, row, :] * (slots[4 + c, row, :] - speed)
                force_rows[pl.ds(c * CAP + r, 1), :] = force
                high, low = split(weights * force)
                terms[c * 32 : (c + 1) * 32, at] = high
                terms[128 + c * 32 : 128 + (c + 1) * 32, at] = low
        return carry

    lax.fori_loop(0, CAP // ranks, owner_step, 0)
    answer[...] = jnp.transpose(force_rows[...])

    def back_copy(peer):
        return pltpu.make_async_remote_copy(
            src_ref=answer.at[pl.ds(peer, 1), :], dst_ref=returned.at[pl.ds(me, 1), :],
            send_sem=back_sem.at[0], recv_sem=back_sem.at[1], device_id=(peer, leaf), device_id_type=MESH,
        )

    def send_back(i, carry):
        back_copy(flow_peer(i)).start()
        return carry

    lax.fori_loop(0, owners - 1, send_back, 0)
    returned[pl.ds(me, 1), :] = answer[pl.ds(me, 1), :]

    def quarter(q):
        part = lax.dot_general(
            hot[pl.ds(pl.multiple_of(q * per_leaf, per_leaf), per_leaf), :], terms[...], NT, preferred_element_type=F32
        )
        part = jnp.transpose(part[:, :LANES] + part[:, LANES:])
        for c in range(3):
            flow_part[q, c * 27 : (c + 1) * 27, :] = part[c * 32 : c * 32 + 27]

    def flow_copy(peer):
        return pltpu.make_async_remote_copy(
            src_ref=flow_part.at[peer], dst_ref=flow_all.at[leaf], send_sem=flow_sem.at[0],
            recv_sem=flow_sem.at[1], device_id=(me, peer), device_id_type=MESH,
        )

    def spread_quarter(i, carry):
        peer = leaf_peer(i)
        quarter(peer)
        flow_copy(peer).start()
        return carry

    lax.fori_loop(0, peers - 1, spread_quarter, 0)
    quarter(leaf)
    flow_all[leaf] = flow_part[leaf]

    pltpu.make_async_remote_copy(
        src_ref=patch_part.at[: peers - 1], dst_ref=patch_all.at[: peers - 1], send_sem=patch_sem.at[0],
        recv_sem=patch_sem.at[1], device_id=(me, leaf_peer(0)), device_id_type=MESH,
    ).wait()
    patch_out[...] = (patch_all[0] + patch_all[1]) + (patch_all[2] + patch_all[3])

    pltpu.make_async_remote_copy(
        src_ref=answer.at[: owners - 1, :], dst_ref=returned.at[: owners - 1, :], send_sem=back_sem.at[0],
        recv_sem=back_sem.at[1], device_id=(flow_peer(0), leaf), device_id_type=MESH,
    ).wait()
    high, low = split(jnp.transpose(returned[...]))
    twice = jnp.concatenate([dest_hot[...], dest_hot[...]], axis=0)
    at_owner = jnp.dot(jnp.concatenate([high, low], axis=1), twice, preferred_element_type=F32)
    rank_hot = lax.broadcasted_iota(jnp.int32, (CAP, points), 0).astype(F32) == rank_row[...]
    for c in range(3):
        fsi = jnp.sum(jnp.where(rank_hot, at_owner[c * CAP : (c + 1) * CAP], 0.0), axis=0, keepdims=True)
        shell_out[c : c + 1, :] = push[c : c + 1, :] - fsi

    pltpu.make_async_remote_copy(
        src_ref=flow_part.at[: peers - 1], dst_ref=flow_all.at[: peers - 1], send_sem=flow_sem.at[0],
        recv_sem=flow_sem.at[1], device_id=(me, leaf_peer(0)), device_id_type=MESH,
    ).wait()
    flow_out[...] = (flow_all[0] + flow_all[1]) + (flow_all[2] + flow_all[3])


def solution(mesh):
    owners, peers = mesh.shape["flow"], mesh.shape["leaf"]

    def per_device(
        vel_coef, gp_block, gp_elem, gp_param, gp_vel, gp_weight, gp_pos, contact_patch, contact_param, patch_ctrl
    ):
        points, elements, patches = gp_elem.shape[0], vel_coef.shape[1], patch_ctrl.shape[1]
        total_slots = CAP * owners
        vmem = pl.BlockSpec(memory_space=pltpu.VMEM)
        return pl.pallas_call(
            kernel,
            out_shape=(
                jax.ShapeDtypeStruct((81, elements // peers), F32),
                jax.ShapeDtypeStruct((3, points), F32),
                jax.ShapeDtypeStruct((27, patches), F32),
            ),
            in_specs=[vmem] * 10,
            out_specs=(vmem,) * 3,
            scratch_shapes=[
                pltpu.VMEM((owners, points), BF16),
                pltpu.VMEM((1, points), F32),
                pltpu.VMEM((16 * CAP, points), BF16),
                pltpu.VMEM((2 * owners, LANES), F32),
                pltpu.VMEM((2 * owners, LANES), F32),
                pltpu.VMEM((8, CAP, LANES), F32),
                pltpu.VMEM((192, elements), BF16),
                pltpu.VMEM((elements, total_slots), BF16),
                pltpu.VMEM((256, total_slots), BF16),
                pltpu.VMEM((LANES, owners), F32),
                pltpu.VMEM((owners, LANES), F32),
                pltpu.VMEM((owners, LANES), F32),
                pltpu.VMEM((peers * patches, points), BF16),
                pltpu.VMEM((LANES, points), BF16),
                pltpu.VMEM((3, points), F32),
                pltpu.VMEM((peers, 27, patches), F32),
                pltpu.VMEM((peers, 27, patches), F32),
                pltpu.VMEM((peers, 27, patches), F32),
                pltpu.VMEM((peers, 81, elements // peers), F32),
                pltpu.VMEM((peers, 81, elements // peers), F32),
                pltpu.SemaphoreType.DMA((2,)),
                pltpu.SemaphoreType.DMA((2,)),
                pltpu.SemaphoreType.DMA((2,)),
                pltpu.SemaphoreType.DMA((2,)),
                pltpu.SemaphoreType.DMA((2,)),
            ],
            compiler_params=pltpu.CompilerParams(
                collective_id=0, has_side_effects=True, vmem_limit_bytes=60 * 1024 * 1024
            ),
        )(
            vel_coef,
            gp_block.reshape(1, points),
            gp_elem.reshape(1, points),
            gp_param,
            gp_vel,
            gp_weight.reshape(1, points),
            gp_pos,
            contact_patch.reshape(1, points),
            contact_param,
            patch_ctrl,
        )

    both = ("flow", "leaf")
    return jax.shard_map(
        per_device,
        mesh=mesh,
        in_specs=(
            P(None, "flow"), P(both, None), P(both), P(None, both), P(None, both),
            P(both), P(None, both), P(both), P(None, both), P(None, both),
        ),
        out_specs=(P(None, both), P(None, both), P(None, both)),
        check_vma=False,
    )
```

time: 229 us -> 53.6 us (0.23); the launches traced: 226 us -> 53.4 us
  local copies, waits for them, and re-layouts: 94.2 us -> 3 us
  other arithmetic: 57.6 us -> 0 us
  Pallas kernels: 0 us -> 49.7 us
  starting transfers between devices: 39.7 us -> 0 us
  waiting for transfers between devices: 29.6 us -> 0 us
  blocking collectives: 3.82 us -> 0 us
    gather x6 -> x0, local copies, waits for them, and re-layouts: 49.8 us -> none  [the longest x4 25.4 us: take_columns(): return jnp.transpose(jnp.transpose(source)[index])]
    pallas_call x0 -> x1, Pallas kernels: none -> 49.7 us  [per_device(): pl.pallas_call(kernel, out_shape=(jax.ShapeDtypeStruct((81, elements // p...]
    all_to_all x5 -> x0, starting transfers between devices: 39.7 us -> none  [the longest x1 19.9 us: per_device(): lax.all_to_all(payload, FLOW, split_axis=2, concat_axis=2, tiled=True)]
    scatter-add x2 -> x0, other arithmetic: 38.2 us -> none  [add_columns(): jnp.zeros((columns, values.shape[0]), jnp.float32).at[index]]
    all_to_all x5 -> x0, waiting for transfers between devices: 29.6 us -> none  [the longest x1 13.9 us: exchange_in_order(): lax.all_to_all(pieces, axes[k], split_axis=k, concat_axis=k, tiled=True)]
    scatter x3 -> x0, local copies, waits for them, and re-layouts: 22.2 us -> none  [the longest x2 14.2 us: pack(): buffer = jnp.full((width, values.shape[0]), filler, jnp.float32).at[slot]...]
    sort x1 -> x0, other arithmetic: 5.74 us -> none  [per_device(): order = jnp.argsort(dest, stable=True)]
    slice x5 -> x0, local copies, waits for them, and re-layouts: 5.63 us -> none  [the longest x2 4.73 us: per_device(): payload[1:]]
  transfers between devices with their start and end apart: 5 -> 0, of which waited for: 3 -> 0; matrix products, arithmetic and copies ran while one was open for 45% -> 0% of each run, Pallas kernels for 0% -> 0%
where the time goes in v1:
time: 53.6 us; the launch traced here: 53.4 us
  Pallas kernels  49.7 us (93%)
  local copies, waits for them, and re-layouts  3 us (6%)
  between operations  0.65 us (1%)
    pallas_call x1, Pallas kernels, per_device(): pl.pallas_call(kernel, out_shape=(jax.ShapeDtypeStruct((81, elements // p...  49.7 us
    unnamed x7, local copies, waits for them, and re-layouts  3 us

profile of v1, /device:TPU:1, one launch (start us, length us, event | category | flops | bytes accessed | tf_op | source)
XLA Modules:
  0.0 53.4 jit_solution(3775809986160901320)
XLA Ops:
  0.6 49.7 %shard_map.121 = (f32[81,512]{1,0:T(8,128)}, f32[3,2048]{1,0:T(4,128)}, f32[27,256]{1,0:T(8,128)}) custom-call(f32[81,2048]{1,0:T(8,128)} %vel_coef.1, s32[1,2048]{1,0:T(1,128)} %bitcast.4, s32[1,2048]{1,0:T(1,128)} %bitcast.5, f32[3,2048]{1,0:T(4,128)} %param_ref.1, f32[3,2048]{1,0:T(4,128)} %vel_ref.1, f32[1,2048]{1,0:T(1,128)} %bitcast.6, ...), custom_call_target="tpu_custom_call" | custom-call | tf_op jit(solution)/shard_map/pallas_call | solution.py:305
  50.4 0.0 copy-start.1
  50.4 1.6 %copy.16 = f32[81,512]{1,0:T(8,128)} copy(f32[81,512]{1,0:T(8,128)} %get-tuple-element.6) | data formatting | bytes 331776
  52.0 0.0 copy-done.1
  52.0 0.0 copy-start
  52.0 0.6 %copy.17 = f32[3,2048]{1,0:T(4,128)} copy(f32[3,2048]{1,0:T(4,128)S(1)} %copy-done.1) | data formatting | bytes 49152
  52.6 0.2 copy-done
  52.8 0.6 %copy.18 = f32[27,256]{1,0:T(8,128)} copy(f32[27,256]{1,0:T(8,128)S(1)} %copy-done) | data formatting | bytes 55296
Async XLA Ops:
  50.4 1.6 %copy-start.1 = (f32[3,2048]{1,0:T(4,128)S(1)}, f32[3,2048]{1,0:T(4,128)}, u32[]{:S(2)}) copy-start(f32[3,2048]{1,0:T(4,128)} %get-tuple-element.7) | copy-start | bytes 73732
  52.0 0.8 %copy-start = (f32[27,256]{1,0:T(8,128)S(1)}, f32[27,256]{1,0:T(8,128)}, u32[]{:S(2)}) copy-start(f32[27,256]{1,0:T(8,128)} %get-tuple-element.8) | copy-start | bytes 82948

commit v2 on v1

v2 whole, which is shorter than its diff:
```python
import jax
import jax.numpy as jnp
from jax import lax
from jax.experimental import pallas as pl
from jax.experimental.pallas import tpu as pltpu
from jax.sharding import PartitionSpec as P

BETA = 1.5
STIFF = 2.0
REACH = 0.5
CAP = 32
LANES = 128
GROUPS = 4
HALF = 96
PITCH = 104
F32 = jnp.float32
BF16 = jnp.bfloat16
MESH = pl.DeviceIdType.MESH
NT = (((1,), (1,)), ((), ()))


def split(x):
    high = x.astype(BF16)
    return high, (x - high.astype(F32)).astype(BF16)


def basis(x):
    return (0.5 * (1.0 - x) ** 2, 0.5 * (1.0 + 2.0 * x - 2.0 * x * x), 0.5 * x * x)


def pick(digit, values):
    return jnp.where(digit == 0, values[0], jnp.where(digit == 1, values[1], values[2]))


def one_hot(row, rows):
    step = min(rows, 256)
    number = lax.broadcasted_iota(jnp.int32, (step, LANES), 0).astype(F32).astype(BF16)
    one, zero = jnp.ones((step, LANES), BF16), jnp.zeros((step, LANES), BF16)
    out = []
    for first in range(0, rows, step):
        near = jnp.broadcast_to(row - float(first), (16, LANES)).astype(BF16)
        near = jnp.concatenate([near] * (step // 16), axis=0)
        out.append(jnp.where(number == near, one, zero))
    return jnp.concatenate(out, axis=0) if len(out) > 1 else out[0]


def kernel(
    vel_coef_hbm, dest_hbm, elem_hbm, param_hbm, vel_hbm, weight_hbm, pos_hbm, patch_hbm, cparam_hbm, ctrl_hbm,
    flow_out, shell_out, patch_out,
    vel_coef, dest_ref, elem_ref, param_ref, vel_ref, weight_ref, pos_ref, patch_ref, cparam_ref, ctrl_ref,
    dest_hot, rank_row, packed, message, received, places, coef, forces, turned, flipped, answer, returned,
    strided, total, contact_terms, push, ctrl_all, patch_part, patch_all,
    in_sem, out_send, out_recv, back_sem, ctrl_sem, patch_sem, place_send, place_recv, force_send, force_recv,
):
    owners, peers = lax.axis_size("flow"), lax.axis_size("leaf")
    me, leaf = lax.axis_index("flow"), lax.axis_index("leaf")
    points = dest_ref.shape[1]
    elements = vel_coef.shape[1]
    per_leaf = elements // peers
    patches = ctrl_ref.shape[1]
    members = owners // GROUPS
    ranks = CAP * members // LANES

    def offset(position):
        return (position + 1) // 2 if position % 2 else (owners - position // 2) % owners

    def ahead_of(position):
        return lax.rem(me + offset(position), owners)

    def behind(position):
        return lax.rem(me + (owners - offset(position)), owners)

    def leaf_peer(i):
        return lax.rem(leaf + i, peers)

    inputs = [
        (dest_hbm, dest_ref), (elem_hbm, elem_ref), (param_hbm, param_ref), (vel_hbm, vel_ref),
        (weight_hbm, weight_ref), (ctrl_hbm, ctrl_ref), (patch_hbm, patch_ref), (pos_hbm, pos_ref),
        (cparam_hbm, cparam_ref), (vel_coef_hbm, vel_coef),
    ]
    fetches = [pltpu.make_async_copy(src, dst, in_sem.at[i]) for i, (src, dst) in enumerate(inputs)]
    for fetch in fetches:
        fetch.start()
    barrier = pltpu.get_barrier_semaphore()
    for position in range(owners - 1, 0, -1):
        pl.semaphore_signal(barrier, inc=1, device_id=(behind(position), leaf), device_id_type=MESH)
    for i in range(1, peers):
        pl.semaphore_signal(barrier, inc=1, device_id=(me, leaf_peer(i)), device_id_type=MESH)

    for fetch in fetches[:6]:
        fetch.wait()
    position = lax.broadcasted_iota(jnp.int32, (owners, 1), 0)
    distance = jnp.where(
        lax.rem(position, 2) == 1, (position + 1) // 2, jnp.where(position == 0, 0, owners - position // 2)
    )
    away = dest_ref[...] - me
    away = jnp.where(away < 0, away + owners, away)
    dest_hot[...] = jnp.where(distance == away, 1.0, 0.0).astype(BF16)
    block = 256
    before = (
        lax.broadcasted_iota(jnp.int32, (block, block), 0) < lax.broadcasted_iota(jnp.int32, (block, block), 1)
    ).astype(F32).astype(BF16)
    carry = jnp.zeros((owners, 1), F32)
    for b in range(points // block):
        part = dest_hot[:, b * block : (b + 1) * block]
        earlier = jnp.dot(part, before, preferred_element_type=F32)
        wide = part.astype(F32)
        rank_row[:, b * block : (b + 1) * block] = jnp.sum(wide * (earlier + carry), axis=0, keepdims=True)
        carry = carry + jnp.sum(wide, axis=1, keepdims=True)

    rank_hot = lax.broadcasted_iota(jnp.int32, (CAP, points), 0).astype(F32) == rank_row[...]
    values = [elem_ref[...].astype(F32)]
    values += [param_ref[i : i + 1, :] for i in range(3)]
    values += [vel_ref[i : i + 1, :] for i in range(3)]
    values += [BETA * weight_ref[...]]
    for v, value in enumerate(values):
        high = value.astype(BF16).astype(F32)
        for h in range(2):
            chosen = rank_hot[h * 16 : (h + 1) * 16]
            at = h * LANES + v * 16
            packed[at : at + 16, :] = jnp.where(chosen, high, 0.0).astype(BF16)
            packed[2 * LANES + at : 2 * LANES + at + 16, :] = jnp.where(chosen, value - high, 0.0).astype(BF16)
    spread = lax.dot_general(packed[...], dest_hot[...], NT, preferred_element_type=F32)
    spread = spread[: 2 * LANES] + spread[2 * LANES :]
    for h in range(2):
        message[pl.ds(h, owners, stride=2), :] = jnp.transpose(spread[h * LANES : (h + 1) * LANES])

    pl.semaphore_wait(barrier, owners - 1 + peers - 1)

    ctrl_copies = [
        pltpu.make_async_remote_copy(
            src_ref=ctrl_ref, dst_ref=ctrl_all.at[leaf], send_sem=ctrl_sem.at[0], recv_sem=ctrl_sem.at[1],
            device_id=(me, leaf_peer(i)), device_id_type=MESH,
        )
        for i in range(1, peers)
    ]
    for copy in ctrl_copies:
        copy.start()
    for position in range(1, owners):
        rows = pl.ds(2 * position, 2)
        pltpu.make_async_remote_copy(
            src_ref=message.at[rows, :], dst_ref=received.at[rows, :], send_sem=out_send,
            recv_sem=out_recv.at[position // members], device_id=(ahead_of(position), leaf), device_id_type=MESH,
        ).start()
    received[0:2, :] = message[0:2, :]
    ctrl_all[leaf] = ctrl_ref[...]

    for fetch in fetches[6:]:
        fetch.wait()
    spare = jnp.zeros((HALF - 81, elements), F32)
    high, low = split(jnp.concatenate([vel_coef[...], spare], axis=0))
    coef[:HALF, :] = high
    coef[HALF:, :] = low

    low_half = lax.broadcasted_iota(jnp.int32, (8, LANES), 1) < LANES // 2
    low_rows = lax.broadcasted_iota(jnp.int32, (members, LANES), 1) < LANES // 2

    def share(buffer, send, recv, g):
        for i in range(1, peers):
            pltpu.make_async_remote_copy(
                src_ref=buffer.at[0, g], dst_ref=buffer.at[i, g], send_sem=send, recv_sem=recv.at[g],
                device_id=(me, leaf_peer(i)), device_id_type=MESH,
            ).start()

    def arrived(buffer, send, recv, g):
        pltpu.make_async_remote_copy(
            src_ref=buffer.at[1:, g], dst_ref=buffer.at[1:, g], send_sem=send, recv_sem=recv.at[g],
            device_id=(me, leaf_peer(1)), device_id_type=MESH,
        ).wait_recv()

    def tile(buffer, source, g, v):
        return buffer[source, g, v * ranks : (v + 1) * ranks, :]

    def gather(g, carry):
        def await_rows(count):
            pltpu.make_async_remote_copy(
                src_ref=message.at[:count, :], dst_ref=received.at[:count, :], send_sem=out_send,
                recv_sem=out_recv.at[g], device_id=(ahead_of(1), leaf), device_id_type=MESH,
            ).wait_recv()

        pl.when(g == 0)(lambda: await_rows(2 * members - 2))
        pl.when(g > 0)(lambda: await_rows(2 * members))
        rows = received[pl.ds(pl.multiple_of(2 * members * g, 2 * members), 2 * members), :]
        rows = jnp.transpose(jnp.concatenate([rows, rows], axis=0))
        values = [jnp.where(low_half, rows[16 * v : 16 * v + 8], rows[16 * v + 8 : 16 * v + 16]) for v in range(8)]
        for v in range(4):
            places[0, g, v * ranks : (v + 1) * ranks, :] = values[v]
        share(places, place_send, place_recv, g)

        for j in range(ranks // 2):
            pair = jnp.concatenate(
                [one_hot(values[0][r : r + 1], elements) for r in (2 * j, 2 * j + 1)], axis=1
            )
            taken = jnp.dot(coef[...], pair, preferred_element_type=F32)
            taken = taken[:HALF] + taken[HALF:]
            for i in range(2):
                at = (2 * j + i) * PITCH
                strided[at : at + HALF, :] = taken[:, i * LANES : (i + 1) * LANES]
        first, second, third = basis(values[1]), basis(values[2]), basis(values[3])
        plane = [x * y for x in second for y in third]
        for c in range(3):
            speed = None
            for a in range(3):
                inner = None
                for k in range(9):
                    term = plane[k] * strided[pl.ds(c * 27 + a * 9 + k, ranks, stride=PITCH), :]
                    inner = term if inner is None else inner + term
                inner = first[a] * inner
                speed = inner if speed is None else speed + inner
            forces[0, g, c * ranks : (c + 1) * ranks, :] = values[7] * (values[4 + c] - speed)
        share(forces, force_send, force_recv, g)

        for c in range(3):
            lower = tile(forces, 0, g, c)
            turned[c * 16 : c * 16 + 8, :] = lower
            turned[c * 16 + 8 : c * 16 + 16, :] = pltpu.roll(lower, LANES // 2, 1)
        flipped[...] = jnp.transpose(turned[...])[: 2 * members, :]
        even = flipped[pl.ds(0, members, stride=2), :]
        odd = flipped[pl.ds(1, members, stride=2), :]
        base = pl.multiple_of(g * members, members)
        answer[pl.ds(base, members), :] = jnp.where(low_rows, even, pltpu.roll(odd, LANES // 2, 1))
        for j in range(members - 1, -1, -1):
            steps = g * (members // 2) + (j + 1) // 2
            partner = lax.rem(me + (owners - steps if j % 2 else steps), owners)

            def reply(j=j, partner=partner):
                row = pl.ds(base + j, 1)
                pltpu.make_async_remote_copy(
                    src_ref=answer.at[row, :], dst_ref=returned.at[row, :], send_sem=back_sem.at[0],
                    recv_sem=back_sem.at[1], device_id=(partner, leaf), device_id_type=MESH,
                ).start()

            if j:
                reply()
            else:
                pl.when(g > 0)(reply)
        return carry

    corner = leaf.astype(F32) * float(per_leaf)

    def scatter(g):
        added = None
        for source in range(peers):
            first, second, third = (basis(tile(places, source, g, v)) for v in (1, 2, 3))
            plane = [x * y for x in second for y in third]
            half = source % 2 * (ranks * PITCH)
            for c in range(3):
                for a in range(3):
                    scaled = tile(forces, source, g, c) * first[a]
                    for k in range(9):
                        strided[pl.ds(half + c * 27 + a * 9 + k, ranks, stride=PITCH), :] = scaled * plane[k]
            near = tile(places, source, g, 0) - corner
            terms, hots = [], []
            for r in range(ranks):
                at = half + r * PITCH
                terms.append(jnp.concatenate(split(strided[at : at + HALF, :]), axis=0))
                hots.append(one_hot(near[r : r + 1], per_leaf))
            part = lax.dot_general(
                jnp.concatenate(hots, axis=1), jnp.concatenate(terms, axis=1), NT, preferred_element_type=F32
            )
            added = part if added is None else added + part
        total[:, : 2 * HALF] += added

    def contact():
        pltpu.make_async_remote_copy(
            src_ref=ctrl_all.at[: peers - 1], dst_ref=ctrl_all.at[: peers - 1], send_sem=ctrl_sem.at[0],
            recv_sem=ctrl_sem.at[1], device_id=(me, leaf_peer(1)), device_id_type=MESH,
        ).wait()
        zero7 = jnp.zeros((7, peers * patches), F32)
        whole = jnp.concatenate([ctrl_all[i] for i in range(peers)], axis=1)
        whole = jnp.concatenate([part for c in range(3) for part in (whole[c * 9 : (c + 1) * 9], zero7)], axis=0)
        ctrl_terms = jnp.concatenate(split(whole), axis=0)
        shell_k = lax.broadcasted_iota(jnp.int32, (16, 1), 0)
        contact_terms[...] = jnp.zeros_like(contact_terms)
        wide = 512

        def partners(start, size):
            return jnp.concatenate(
                [
                    one_hot(patch_ref[:, at : at + LANES].astype(F32), peers * patches)
                    for at in range(start, start + size, LANES)
                ],
                axis=1,
            )

        for j in range(points // wide):
            cols = slice(j * wide, (j + 1) * wide)
            taken = jnp.dot(ctrl_terms, partners(j * wide, wide), preferred_element_type=F32)
            taken = taken[:48] + taken[48:]
            weights = pick(shell_k // 3, basis(cparam_ref[0:1, cols])) * pick(
                lax.rem(shell_k, 3), basis(cparam_ref[1:2, cols])
            )
            weights = jnp.where(shell_k < 9, weights, 0.0)
            gap = [
                pos_ref[c : c + 1, cols] - jnp.sum(taken[c * 16 : (c + 1) * 16] * weights, axis=0, keepdims=True)
                for c in range(3)
            ]
            scale = STIFF / (1.0 + (gap[0] * gap[0] + gap[1] * gap[1] + gap[2] * gap[2]) / (REACH * REACH))
            for c in range(3):
                fc = scale * gap[c]
                push[c : c + 1, cols] = fc
                high, low = split(-(weights * fc))
                contact_terms[c * 16 : (c + 1) * 16, cols] = high
                contact_terms[64 + c * 16 : 64 + (c + 1) * 16, cols] = low
        reaction = lax.dot_general(partners(0, points), contact_terms[...], NT, preferred_element_type=F32)
        reaction = jnp.transpose(reaction)
        reaction = reaction[:48] + reaction[64:112]
        for q in range(peers):
            for c in range(3):
                patch_part[q, c * 9 : (c + 1) * 9, :] = reaction[c * 16 : c * 16 + 9, q * patches : (q + 1) * patches]
        for i in range(1, peers):
            pltpu.make_async_remote_copy(
                src_ref=patch_part.at[leaf_peer(i)], dst_ref=patch_all.at[leaf], send_sem=patch_sem.at[0],
                recv_sem=patch_sem.at[1], device_id=(me, leaf_peer(i)), device_id_type=MESH,
            ).start()
        patch_all[leaf] = patch_part[leaf]

    total[...] = jnp.zeros_like(total)
    turned[...] = jnp.zeros_like(turned)
    lax.fori_loop(0, GROUPS, gather, 0)
    returned[0:1, :] = answer[0:1, :]
    contact()
    strided[...] = jnp.zeros_like(strided)

    def gathered(g, carry):
        arrived(places, place_send, place_recv, g)
        arrived(forces, force_send, force_recv, g)
        scatter(g)
        return carry

    lax.fori_loop(0, GROUPS, gathered, 0)
    sums = jnp.transpose(total[...])
    flow_out[...] = sums[:81] + sums[HALF : HALF + 81]

    pltpu.make_async_remote_copy(
        src_ref=patch_part.at[: peers - 1], dst_ref=patch_all.at[: peers - 1], send_sem=patch_sem.at[0],
        recv_sem=patch_sem.at[1], device_id=(me, leaf_peer(1)), device_id_type=MESH,
    ).wait()
    patch_out[...] = (patch_all[0] + patch_all[1]) + (patch_all[2] + patch_all[3])

    pltpu.make_async_remote_copy(
        src_ref=answer.at[: owners - 1, :], dst_ref=returned.at[: owners - 1, :], send_sem=back_sem.at[0],
        recv_sem=back_sem.at[1], device_id=(ahead_of(1), leaf), device_id_type=MESH,
    ).wait()
    high, low = split(jnp.transpose(returned[...]))
    twice = jnp.concatenate([dest_hot[...], dest_hot[...]], axis=0)
    at_owner = jnp.dot(jnp.concatenate([high, low], axis=1), twice, preferred_element_type=F32)
    number = lax.broadcasted_iota(jnp.int32, (16, points), 0).astype(F32)
    for c in range(3):
        fsi = jnp.zeros((1, points), F32)
        for h in range(2):
            at = h * (LANES // 2) + c * 16
            mine = number == rank_row[...] - float(16 * h)
            fsi = fsi + jnp.sum(jnp.where(mine, at_owner[at : at + 16], 0.0), axis=0, keepdims=True)
        shell_out[c : c + 1, :] = push[c : c + 1, :] - fsi

    pltpu.make_async_remote_copy(
        src_ref=message.at[: 2 * (owners - 1), :], dst_ref=received.at[: 2 * (owners - 1), :], send_sem=out_send,
        recv_sem=out_recv.at[0], device_id=(ahead_of(1), leaf), device_id_type=MESH,
    ).wait_send()
    for buffer, send, recv in ((places, place_send, place_recv), (forces, force_send, force_recv)):
        pltpu.make_async_remote_copy(
            src_ref=buffer.at[1:], dst_ref=buffer.at[1:], send_sem=send, recv_sem=recv.at[0],
            device_id=(me, leaf_peer(1)), device_id_type=MESH,
        ).wait_send()


def finish(flow_in, shell_in, patch_in, flow_out, shell_out, patch_out):
    flow_out[...] = flow_in[...]
    shell_out[...] = shell_in[...]
    patch_out[...] = patch_in[...]


def solution(mesh):
    owners, peers = mesh.shape["flow"], mesh.shape["leaf"]

    def per_device(
        vel_coef, gp_block, gp_elem, gp_param, gp_vel, gp_weight, gp_pos, contact_patch, contact_param, patch_ctrl
    ):
        points, elements, patches = gp_elem.shape[0], vel_coef.shape[1], patch_ctrl.shape[1]
        per_leaf = elements // peers
        ranks = CAP * owners // GROUPS // LANES
        vmem = pl.BlockSpec(memory_space=pltpu.VMEM)
        outs = (
            jax.ShapeDtypeStruct((81, per_leaf), F32),
            jax.ShapeDtypeStruct((3, points), F32),
            jax.ShapeDtypeStruct((27, patches), F32),
        )
        arguments = (
            vel_coef,
            gp_block.reshape(1, points),
            gp_elem.reshape(1, points),
            gp_param,
            gp_vel,
            gp_weight.reshape(1, points),
            gp_pos,
            contact_patch.reshape(1, points),
            contact_param,
            patch_ctrl,
        )
        results = pl.pallas_call(
            kernel,
            out_shape=outs,
            in_specs=[pl.BlockSpec(memory_space=pl.ANY)] * 10,
            out_specs=(vmem,) * 3,
            scratch_shapes=[pltpu.VMEM(x.shape, x.dtype) for x in arguments]
            + [
                pltpu.VMEM((owners, points), BF16),
                pltpu.VMEM((1, points), F32),
                pltpu.VMEM((4 * LANES, points), BF16),
                pltpu.VMEM((2 * owners, LANES), F32),
                pltpu.VMEM((2 * owners, LANES), F32),
                pltpu.VMEM((peers, GROUPS, 4 * ranks, LANES), F32),
                pltpu.VMEM((2 * HALF, elements), BF16),
                pltpu.VMEM((peers, GROUPS, 3 * ranks, LANES), F32),
                pltpu.VMEM((LANES, LANES), F32),
                pltpu.VMEM((2 * owners // GROUPS, LANES), F32),
                pltpu.VMEM((owners, LANES), F32),
                pltpu.VMEM((owners, LANES), F32),
                pltpu.VMEM((2 * ranks * PITCH, LANES), F32),
                pltpu.VMEM((per_leaf, 2 * LANES), F32),
                pltpu.VMEM((LANES, points), BF16),
                pltpu.VMEM((3, points), F32),
                pltpu.VMEM((peers, 27, patches), F32),
                pltpu.VMEM((peers, 27, patches), F32),
                pltpu.VMEM((peers, 27, patches), F32),
                pltpu.SemaphoreType.DMA((10,)),
                pltpu.SemaphoreType.DMA,
                pltpu.SemaphoreType.DMA((GROUPS,)),
                pltpu.SemaphoreType.DMA((2,)),
                pltpu.SemaphoreType.DMA((2,)),
                pltpu.SemaphoreType.DMA((2,)),
                pltpu.SemaphoreType.DMA,
                pltpu.SemaphoreType.DMA((GROUPS,)),
                pltpu.SemaphoreType.DMA,
                pltpu.SemaphoreType.DMA((GROUPS,)),
            ],
            compiler_params=pltpu.CompilerParams(
                collective_id=0, has_side_effects=True, vmem_limit_bytes=60 * 1024 * 1024
            ),
        )(*arguments)
        return pl.pallas_call(finish, out_shape=outs, in_specs=[vmem] * 3, out_specs=(vmem,) * 3)(*results)

    both = ("flow", "leaf")
    return jax.shard_map(
        per_device,
        mesh=mesh,
        in_specs=(
            P(None, "flow"), P(both, None), P(both), P(None, both), P(None, both),
            P(both), P(None, both), P(both), P(None, both), P(None, both),
        ),
        out_specs=(P(None, both), P(None, both), P(None, both)),
        check_vma=False,
    )
```

time: 53.6 us -> 43.2 us (0.81)
  Pallas kernels: 49.7 us -> 42.5 us
  local copies, waits for them, and re-layouts: 3 us -> 0 us
    pallas_call x1 -> x2, Pallas kernels: 49.7 us -> 42.5 us  [the longest x1 40.8 us: per_device(): pl.pallas_call(kernel, out_shape=outs, in_specs=[pl.BlockSpec(memory_spac...]
    unnamed x7 -> x0, local copies, waits for them, and re-layouts: 3 us -> none
where the time goes in v2:
time: 43.2 us; the launch traced here: 43.1 us
  Pallas kernels  42.5 us (98%)
  between operations  0.64 us (1%)
    pallas_call x1, Pallas kernels, per_device(): pl.pallas_call(kernel, out_shape=outs, in_specs=[pl.BlockSpec(memory_spac...  40.8 us
    pallas_call x1, Pallas kernels, per_device(): pl.pallas_call(finish, out_shape=outs, in_specs=[vmem] * 3, out_specs=(vm...  1.63 us

profile of v2, /device:TPU:1, one launch (start us, length us, event | category | flops | bytes accessed | tf_op | source)
XLA Modules:
  0.0 43.1 jit_solution(11869273160622602473)
XLA Ops:
  0.6 40.8 %shard_map.121 = (f32[81,512]{1,0:T(8,128)}, f32[3,2048]{1,0:T(4,128)}, f32[27,256]{1,0:T(8,128)}) custom-call(f32[81,2048]{1,0:T(8,128)} %vel_coef_hbm.1, s32[1,2048]{1,0:T(1,128)} %bitcast.4, s32[1,2048]{1,0:T(1,128)} %bitcast.5, f32[3,2048]{1,0:T(4,128)} %param_hbm.1, f32[3,2048]{1,0:T(4,128)} %vel_hbm.1, f32[1,2048]{1,0:T(1,128)} %bitcast.6, ...), custom_call_target="tpu_custom_call" | custom-call | tf_op jit(solution)/shard_map/pallas_call | solution.py:401
  41.5 1.6 %shard_map.122 = (f32[81,512]{1,0:T(8,128)}, f32[3,2048]{1,0:T(4,128)}, f32[27,256]{1,0:T(8,128)}) custom-call(f32[81,512]{1,0:T(8,128)} %get-tuple-element.6.flow_in, f32[3,2048]{1,0:T(4,128)} %get-tuple-element.7.shell_in, f32[27,256]{1,0:T(8,128)} %get-tuple-element.8.patch_in), custom_call_target="tpu_custom_call" | custom-call | tf_op jit(solution)/shard_map/pallas_call | solution.py:442

commit v3 on v2

--- a/solution.py
+++ b/solution.py
@@ -136,7 +136,7 @@
     ]
     for copy in ctrl_copies:
         copy.start()
-    for position in range(1, owners):
+    for position in [g * members + j for g in (3, 0, 2, 1) for j in range(members - 1, -1, -1) if g or j]:
         rows = pl.ds(2 * position, 2)
         pltpu.make_async_remote_copy(
             src_ref=message.at[rows, :], dst_ref=received.at[rows, :], send_sem=out_send,
@@ -171,7 +171,12 @@
     def tile(buffer, source, g, v):
         return buffer[source, g, v * ranks : (v + 1) * ranks, :]
 
-    def gather(g, carry):
+    def turn(i):
+        return lax.rem(GROUPS - i, GROUPS)
+
+    def gather(i, carry):
+        g = turn(i)
+
         def await_rows(count):
             pltpu.make_async_remote_copy(
                 src_ref=message.at[:count, :], dst_ref=received.at[:count, :], send_sem=out_send,
@@ -317,12 +322,13 @@
 
     total[...] = jnp.zeros_like(total)
     turned[...] = jnp.zeros_like(turned)
+    contact()
     lax.fori_loop(0, GROUPS, gather, 0)
     returned[0:1, :] = answer[0:1, :]
-    contact()
     strided[...] = jnp.zeros_like(strided)
 
-    def gathered(g, carry):
+    def gathered(i, carry):
+        g = turn(i)
         arrived(places, place_send, place_recv, g)
         arrived(forces, force_send, force_recv, g)
         scatter(g)
@@ -365,10 +371,15 @@
         ).wait_send()
 
 
-def finish(flow_in, shell_in, patch_in, flow_out, shell_out, patch_out):
-    flow_out[...] = flow_in[...]
-    shell_out[...] = shell_in[...]
-    patch_out[...] = patch_in[...]
+def finish(flow_in, shell_in, patch_in, flow_out, shell_out, patch_out, sems):
+    copies = [
+        pltpu.make_async_copy(src, dst, sems.at[i])
+        for i, (src, dst) in enumerate(((flow_in, flow_out), (shell_in, shell_out), (patch_in, patch_out)))
+    ]
+    for copy in copies:
+        copy.start()
+    for copy in copies:
+        copy.wait()
 
 
 def solution(mesh):
@@ -400,7 +411,7 @@
         )
         results = pl.pallas_call(
             kernel,
-            out_shape=outs,
+            out_shape=tuple(pltpu.VMEM(x.shape, x.dtype) for x in outs),
             in_specs=[pl.BlockSpec(memory_space=pl.ANY)] * 10,
             out_specs=(vmem,) * 3,
             scratch_shapes=[pltpu.VMEM(x.shape, x.dtype) for x in arguments]
@@ -439,7 +450,15 @@
                 collective_id=0, has_side_effects=True, vmem_limit_bytes=60 * 1024 * 1024
             ),
         )(*arguments)
-        return pl.pallas_call(finish, out_shape=outs, in_specs=[vmem] * 3, out_specs=(vmem,) * 3)(*results)
+        return pl.pallas_call(
+            finish,
+            out_shape=outs,
+            in_specs=[vmem] * 3,
+            out_specs=(pl.BlockSpec(memory_space=pl.ANY),) * 3,
+            scratch_shapes=[pltpu.SemaphoreType.DMA((3,))],
+        )(
+            *[pltpu.with_memory_space_constraint(x, pltpu.VMEM) for x in results]
+        )
 
     both = ("flow", "leaf")
     return jax.shard_map(

time: 43.2 us -> 39.9 us (0.924)
  Pallas kernels: 42.5 us -> 39.2 us
    pallas_call x2, Pallas kernels: 42.5 us -> 39.2 us  [the longest x1 38.4 us: per_device(): pl.pallas_call(kernel, out_shape=tuple((pltpu.VMEM(x.shape, x.dtype) for...]
where the time goes in v3:
time: 39.9 us; the launch traced here: 39.8 us
  Pallas kernels  39.2 us (98%)
  between operations  0.64 us (2%)
    pallas_call x1, Pallas kernels, per_device(): pl.pallas_call(kernel, out_shape=tuple((pltpu.VMEM(x.shape, x.dtype) for...  38.4 us

profile of v3, /device:TPU:1, one launch (start us, length us, event | category | flops | bytes accessed | tf_op | source)
XLA Modules:
  0.0 39.8 jit_solution(16968989188441108972)
XLA Ops:
  0.6 38.4 %shard_map.121 = (f32[81,512]{1,0:T(8,128)S(1)}, f32[3,2048]{1,0:T(4,128)S(1)}, f32[27,256]{1,0:T(8,128)S(1)}) custom-call(f32[81,2048]{1,0:T(8,128)} %vel_coef_hbm.1, s32[1,2048]{1,0:T(1,128)} %bitcast.4, s32[1,2048]{1,0:T(1,128)} %bitcast.5, f32[3,2048]{1,0:T(4,128)} %param_hbm.1, f32[3,2048]{1,0:T(4,128)} %vel_hbm.1, f32[1,2048]{1,0:T(1,128)} %bitcast.6, ...), custom_call_target="tpu_custom_call" | custom-call | tf_op jit(solution)/shard_map/pallas_call | solution.py:412
  39.1 0.7 %shard_map.122 = (f32[81,512]{1,0:T(8,128)}, f32[3,2048]{1,0:T(4,128)}, f32[27,256]{1,0:T(8,128)}) custom-call(f32[81,512]{1,0:T(8,128)S(1)} %get-tuple-element.6.flow_in, f32[3,2048]{1,0:T(4,128)S(1)} %get-tuple-element.7.shell_in, f32[27,256]{1,0:T(8,128)S(1)} %get-tuple-element.8.patch_in), custom_call_target="tpu_custom_call" | custom-call | tf_op jit(solution)/shard_map/pallas_call | solution.py:453

commit v4 on v3

--- a/solution.py
+++ b/solution.py
@@ -136,7 +136,7 @@
     ]
     for copy in ctrl_copies:
         copy.start()
-    for position in [g * members + j for g in (3, 0, 2, 1) for j in range(members - 1, -1, -1) if g or j]:
+    for position in [g * members + j for g in (0, 3, 2, 1) for j in range(members - 1, -1, -1) if g or j]:
         rows = pl.ds(2 * position, 2)
         pltpu.make_async_remote_copy(
             src_ref=message.at[rows, :], dst_ref=received.at[rows, :], send_sem=out_send,
@@ -173,98 +173,6 @@
 
     def turn(i):
         return lax.rem(GROUPS - i, GROUPS)
-
-    def gather(i, carry):
-        g = turn(i)
-
-        def await_rows(count):
-            pltpu.make_async_remote_copy(
-                src_ref=message.at[:count, :], dst_ref=received.at[:count, :], send_sem=out_send,
-                recv_sem=out_recv.at[g], device_id=(ahead_of(1), leaf), device_id_type=MESH,
-            ).wait_recv()
-
-        pl.when(g == 0)(lambda: await_rows(2 * members - 2))
-        pl.when(g > 0)(lambda: await_rows(2 * members))
-        rows = received[pl.ds(pl.multiple_of(2 * members * g, 2 * members), 2 * members), :]
-        rows = jnp.transpose(jnp.concatenate([rows, rows], axis=0))
-        values = [jnp.where(low_half, rows[16 * v : 16 * v + 8], rows[16 * v + 8 : 16 * v + 16]) for v in range(8)]
-        for v in range(4):
-            places[0, g, v * ranks : (v + 1) * ranks, :] = values[v]
-        share(places, place_send, place_recv, g)
-
-        for j in range(ranks // 2):
-            pair = jnp.concatenate(
-                [one_hot(values[0][r : r + 1], elements) for r in (2 * j, 2 * j + 1)], axis=1
-            )
-            taken = jnp.dot(coef[...], pair, preferred_element_type=F32)
-            taken = taken[:HALF] + taken[HALF:]
-            for i in range(2):
-                at = (2 * j + i) * PITCH
-                strided[at : at + HALF, :] = taken[:, i * LANES : (i + 1) * LANES]
-        first, second, third = basis(values[1]), basis(values[2]), basis(values[3])
-        plane = [x * y for x in second for y in third]
-        for c in range(3):
-            speed = None
-            for a in range(3):
-                inner = None
-                for k in range(9):
-                    term = plane[k] * strided[pl.ds(c * 27 + a * 9 + k, ranks, stride=PITCH), :]
-                    inner = term if inner is None else inner + term
-                inner = first[a] * inner
-                speed = inner if speed is None else speed + inner
-            forces[0, g, c * ranks : (c + 1) * ranks, :] = values[7] * (values[4 + c] - speed)
-        share(forces, force_send, force_recv, g)
-
-        for c in range(3):
-            lower = tile(forces, 0, g, c)
-            turned[c * 16 : c * 16 + 8, :] = lower
-            turned[c * 16 + 8 : c * 16 + 16, :] = pltpu.roll(lower, LANES // 2, 1)
-        flipped[...] = jnp.transpose(turned[...])[: 2 * members, :]
-        even = flipped[pl.ds(0, members, stride=2), :]
-        odd = flipped[pl.ds(1, members, stride=2), :]
-        base = pl.multiple_of(g * members, members)
-        answer[pl.ds(base, members), :] = jnp.where(low_rows, even, pltpu.roll(odd, LANES // 2, 1))
-        for j in range(members - 1, -1, -1):
-            steps = g * (members // 2) + (j + 1) // 2
-            partner = lax.rem(me + (owners - steps if j % 2 else steps), owners)
-
-            def reply(j=j, partner=partner):
-                row = pl.ds(base + j, 1)
-                pltpu.make_async_remote_copy(
-                    src_ref=answer.at[row, :], dst_ref=returned.at[row, :], send_sem=back_sem.at[0],
-                    recv_sem=back_sem.at[1], device_id=(partner, leaf), device_id_type=MESH,
-                ).start()
-
-            if j:
-                reply()
-            else:
-                pl.when(g > 0)(reply)
-        return carry
-
-    corner = leaf.astype(F32) * float(per_leaf)
-
-    def scatter(g):
-        added = None
-        for source in range(peers):
-            first, second, third = (basis(tile(places, source, g, v)) for v in (1, 2, 3))
-            plane = [x * y for x in second for y in third]
-            half = source % 2 * (ranks * PITCH)
-            for c in range(3):
-                for a in range(3):
-                    scaled = tile(forces, source, g, c) * first[a]
-                    for k in range(9):
-                        strided[pl.ds(half + c * 27 + a * 9 + k, ranks, stride=PITCH), :] = scaled * plane[k]
-            near = tile(places, source, g, 0) - corner
-            terms, hots = [], []
-            for r in range(ranks):
-                at = half + r * PITCH
-                terms.append(jnp.concatenate(split(strided[at : at + HALF, :]), axis=0))
-                hots.append(one_hot(near[r : r + 1], per_leaf))
-            part = lax.dot_general(
-                jnp.concatenate(hots, axis=1), jnp.concatenate(terms, axis=1), NT, preferred_element_type=F32
-            )
-            added = part if added is None else added + part
-        total[:, : 2 * HALF] += added
 
     def contact():
         pltpu.make_async_remote_copy(
@@ -320,9 +228,101 @@
             ).start()
         patch_all[leaf] = patch_part[leaf]
 
+    def gather(order, carry):
+        g = turn(order)
+
+        def await_rows(count):
+            pltpu.make_async_remote_copy(
+                src_ref=message.at[:count, :], dst_ref=received.at[:count, :], send_sem=out_send,
+                recv_sem=out_recv.at[g], device_id=(ahead_of(1), leaf), device_id_type=MESH,
+            ).wait_recv()
+
+        pl.when(g == 0)(lambda: await_rows(2 * members - 2))
+        pl.when(g > 0)(lambda: await_rows(2 * members))
+        rows = received[pl.ds(pl.multiple_of(2 * members * g, 2 * members), 2 * members), :]
+        rows = jnp.transpose(jnp.concatenate([rows, rows], axis=0))
+        values = [jnp.where(low_half, rows[16 * v : 16 * v + 8], rows[16 * v + 8 : 16 * v + 16]) for v in range(8)]
+        for v in range(4):
+            places[0, g, v * ranks : (v + 1) * ranks, :] = values[v]
+        share(places, place_send, place_recv, g)
+
+        for j in range(ranks // 2):
+            pair = jnp.concatenate(
+                [one_hot(values[0][r : r + 1], elements) for r in (2 * j, 2 * j + 1)], axis=1
+            )
+            taken = jnp.dot(coef[...], pair, preferred_element_type=F32)
+            taken = taken[:HALF] + taken[HALF:]
+            for side in range(2):
+                at = (2 * j + side) * PITCH
+                strided[at : at + HALF, :] = taken[:, side * LANES : (side + 1) * LANES]
+        first, second, third = basis(values[1]), basis(values[2]), basis(values[3])
+        plane = [x * y for x in second for y in third]
+        for c in range(3):
+            speed = None
+            for a in range(3):
+                inner = None
+                for k in range(9):
+                    term = plane[k] * strided[pl.ds(c * 27 + a * 9 + k, ranks, stride=PITCH), :]
+                    inner = term if inner is None else inner + term
+                inner = first[a] * inner
+                speed = inner if speed is None else speed + inner
+            forces[0, g, c * ranks : (c + 1) * ranks, :] = values[7] * (values[4 + c] - speed)
+        share(forces, force_send, force_recv, g)
+
+        for c in range(3):
+            lower = tile(forces, 0, g, c)
+            turned[c * 16 : c * 16 + 8, :] = lower
+            turned[c * 16 + 8 : c * 16 + 16, :] = pltpu.roll(lower, LANES // 2, 1)
+        flipped[...] = jnp.transpose(turned[...])[: 2 * members, :]
+        even = flipped[pl.ds(0, members, stride=2), :]
+        odd = flipped[pl.ds(1, members, stride=2), :]
+        base = pl.multiple_of(g * members, members)
+        answer[pl.ds(base, members), :] = jnp.where(low_rows, even, pltpu.roll(odd, LANES // 2, 1))
+        for j in range(members - 1, -1, -1):
+            steps = g * (members // 2) + (j + 1) // 2
+            partner = lax.rem(me + (owners - steps if j % 2 else steps), owners)
+
+            def reply(j=j, partner=partner):
+                row = pl.ds(base + j, 1)
+                pltpu.make_async_remote_copy(
+                    src_ref=answer.at[row, :], dst_ref=returned.at[row, :], send_sem=back_sem.at[0],
+                    recv_sem=back_sem.at[1], device_id=(partner, leaf), device_id_type=MESH,
+                ).start()
+
+            if j:
+                reply()
+            else:
+                pl.when(g > 0)(reply)
+        pl.when(order == 0)(contact)
+        return carry
+
+    corner = leaf.astype(F32) * float(per_leaf)
+
+    def scatter(g):
+        added = None
+        for source in range(peers):
+            first, second, third = (basis(tile(places, source, g, v)) for v in (1, 2, 3))
+            plane = [x * y for x in second for y in third]
+            half = source % 2 * (ranks * PITCH)
+            for c in range(3):
+                for a in range(3):
+                    scaled = tile(forces, source, g, c) * first[a]
+                    for k in range(9):
+                        strided[pl.ds(half + c * 27 + a * 9 + k, ranks, stride=PITCH), :] = scaled * plane[k]
+            near = tile(places, source, g, 0) - corner
+            terms, hots = [], []
+            for r in range(ranks):
+                at = half + r * PITCH
+                terms.append(jnp.concatenate(split(strided[at : at + HALF, :]), axis=0))
+                hots.append(one_hot(near[r : r + 1], per_leaf))
+            part = lax.dot_general(
+                jnp.concatenate(hots, axis=1), jnp.concatenate(terms, axis=1), NT, preferred_element_type=F32
+            )
+            added = part if added is None else added + part
+        total[:, : 2 * HALF] += added
+
     total[...] = jnp.zeros_like(total)
     turned[...] = jnp.zeros_like(turned)
-    contact()
     lax.fori_loop(0, GROUPS, gather, 0)
     returned[0:1, :] = answer[0:1, :]
     strided[...] = jnp.zeros_like(strided)

time: 39.9 us -> 40.3 us (1.010)
  no operation moved by 1% of the time
where the time goes in v4:
time: 40.3 us; the launch traced here: 40.1 us
  Pallas kernels  39.5 us (98%)
  between operations  0.64 us (2%)
    pallas_call x1, Pallas kernels, per_device(): pl.pallas_call(kernel, out_shape=tuple((pltpu.VMEM(x.shape, x.dtype) for...  38.8 us

profile of v4, /device:TPU:1, one launch (start us, length us, event | category | flops | bytes accessed | tf_op | source)
XLA Modules:
  0.0 40.1 jit_solution(12148648814863218782)
XLA Ops:
  0.6 38.8 %shard_map.121 = (f32[81,512]{1,0:T(8,128)S(1)}, f32[3,2048]{1,0:T(4,128)S(1)}, f32[27,256]{1,0:T(8,128)S(1)}) custom-call(f32[81,2048]{1,0:T(8,128)} %vel_coef_hbm.1, s32[1,2048]{1,0:T(1,128)} %bitcast.4, s32[1,2048]{1,0:T(1,128)} %bitcast.5, f32[3,2048]{1,0:T(4,128)} %param_hbm.1, f32[3,2048]{1,0:T(4,128)} %vel_hbm.1, f32[1,2048]{1,0:T(1,128)} %bitcast.6, ...), custom_call_target="tpu_custom_call" | custom-call | tf_op jit(solution)/shard_map/pallas_call | solution.py:412
  39.4 0.7 %shard_map.122 = (f32[81,512]{1,0:T(8,128)}, f32[3,2048]{1,0:T(4,128)}, f32[27,256]{1,0:T(8,128)}) custom-call(f32[81,512]{1,0:T(8,128)S(1)} %get-tuple-element.6.flow_in, f32[3,2048]{1,0:T(4,128)S(1)} %get-tuple-element.7.shell_in, f32[27,256]{1,0:T(8,128)S(1)} %get-tuple-element.8.patch_in), custom_call_target="tpu_custom_call" | custom-call | tf_op jit(solution)/shard_map/pallas_call | solution.py:453
